TPU v7x, 32 devices: a whole 2x2x4 slice. The times are simulated.
32 devices in a mesh: rep: 4 (over z), fsdp: 2 (over x), tp: 4 (over y, core).
Axes of the slice: x: 2, y: 2, z: 4, core: 2. Of those that a mesh axis runs over, the one named last changes fastest.
Arguments:
- gate_pre: bfloat16 [1024, 14848], P(('rep', 'fsdp'), 'tp'), may hold values from -6 to 6
- up_pre: bfloat16 [1024, 14848], P(('rep', 'fsdp'), 'tp'), may hold values from -30 to 30
- out_grad: bfloat16 [1024, 4096], P(('rep', 'fsdp')), may hold values from -30 to 30
Outputs:
- down_grad: bfloat16 [4096, 14848], P('fsdp', 'tp')
All inputs are finite; a program needn't handle non-finite values.
Results may differ from a plain program's by a relative error of at most 0.02.
Values may be sent and summed in bfloat16 or wider, within the bound.
A program may use at most 128 MiB of HBM per device.

v0:
```python
import jax
import jax.numpy as jnp
from jax import lax
from jax.sharding import PartitionSpec as P


def on_device(gate_pre, up_pre, out_grad):
    hidden = (jax.nn.silu(gate_pre.astype(jnp.float32)) * up_pre.astype(jnp.float32)).astype(
        jnp.bfloat16
    )
    feature_rows = out_grad.shape[1] // lax.axis_size("fsdp")
    block_rows = out_grad.shape[0]
    spread = lax.all_to_all(out_grad, "fsdp", split_axis=1, concat_axis=0, tiled=True)

    def advance(running, paired):
        grad_rows, hidden_rows = paired
        partial_term = jnp.dot(grad_rows.T, hidden_rows, preferred_element_type=jnp.float32)
        return (running + partial_term.astype(jnp.bfloat16).astype(jnp.float32), None)

    starting = jnp.zeros((feature_rows, hidden.shape[1]), jnp.float32)
    running = starting
    portion = lax.all_gather(hidden, "fsdp", axis=0, tiled=True)
    row_count = portion.shape[0]
    blocks = row_count // block_rows
    grad_rows = spread
    running, unused = lax.scan(
        advance,
        running,
        (
            grad_rows.reshape(blocks, block_rows, grad_rows.shape[1]),
            portion.reshape(blocks, block_rows, portion.shape[1]),
        ),
    )
    summed = lax.psum(running.astype(jnp.bfloat16), "rep").astype(jnp.float32)
    square_total = lax.psum(jnp.sum(summed * summed), ("fsdp", "tp"))
    entry_count = summed.shape[0] * lax.axis_size("fsdp") * summed.shape[1] * lax.axis_size("tp")
    factor = 1.0 / jnp.sqrt(square_total / entry_count + 1e-06)
    return (summed * factor).astype(jnp.bfloat16)


def solution(mesh):
    return jax.shard_map(
        on_device,
        mesh=mesh,
        in_specs=(P(("rep", "fsdp"), "tp"), P(("rep", "fsdp"), "tp"), P(("rep", "fsdp"), None)),
        out_specs=P("fsdp", "tp"),
        check_vma=False,
    )
```

profile of v0, /device:TPU:0, one launch (start us, length us, event | category | flops | bytes accessed | tf_op | source)
XLA Modules:
  0.0 660.7 jit_solution(3080684873038719467)
XLA Ops:
  6.5 0.0 all-gather.2.cloned.1.call-start
  6.5 3.0 fusion.11
  9.5 0.0 all-gather.2.cloned.1.call-update
  9.6 2.3 copy.4
  11.8 4.2 all-to-all-start
  16.1 0.0 all-reduce.2.cloned.1.call-start
  16.1 23.0 %all-to-all-done = bf16[128,2,2048]{0,2,1:T(8,128)(2,1)S(1)} async-done(((bf16[128,2,2048]{0,2,1:T(8,128)(2,1)}), bf16[128,2,2048]{0,2,1:T(8,128)(2,1)S(1)}, u32[]{:S(2)}, u32[]{:S(2)}) %all-to-all-start) | async-done | bytes 1048608 | tf_op jit(solution)/shard_map/all_to_all | solution.py:13
  39.1 12.0 %all-gather.2.cloned.1.call-done = bf16[256,3712]{1,0:T(8,128)(2,1)} async-done(((bf16[128,3712]{1,0:T(8,128)(2,1)}), bf16[256,3712]{1,0:T(8,128)(2,1)}) %all-gather.2.cloned.1.call-update) | async-done | bytes 1900560 | tf_op jit(solution)/shard_map/all_gather | solution.py:22
  51.1 35.5 %while.11 = (s32[]{:T(128)}, f32[2048,3712]{1,0:T(8,128)}, bf16[2,128,2048]{1,2,0:T(8,128)(2,1)S(1)}, bf16[2,128,3712]{2,1,0:T(8,128)(2,1)}, s32[]{:T(128)}, /*index=5*/s32[]{:T(128)}) while((s32[]{:T(128)}, f32[2048,3712]{1,0:T(8,128)}, bf16[2,128,2048]{1,2,0:T(8,128)(2,1)S(1)}, bf16[2,128,3712]{2,1,0:T(8,128)(2,1)}, s32[]{:T(128)}, ...), condition=%wide.region_1.2_spmd.clone, body=%wide.region_0.1_spmd.clone.sunk | while | flops 1976565760 | bytes 62293588 | solution.py:26
  51.1 12.6 %select_add_fusion.2 = f32[2048,3712]{1,0:T(8,128)} fusion(f32[2048,3712]{1,0:T(8,128)} %get-tuple-element.87, pred[]{:T(512)S(6)} %compare.3, bf16[2,128,3712]{2,1,0:T(8,128)(2,1)} %get-tuple-element.95, s32[]{:T(128)S(6)} %copy.9, bf16[2,128,2048]{1,2,0:T(8,128)(2,1)S(1)} %get-tuple-element.94), kind=kOutput, calls=%fused_computation.clone.1 | convolution fusion | flops 1976565760 | bytes 62293504 | tf_op jit(solution)/shard_map/while/body/eval_jaxpr/dot_general | solution.py:17
  63.7 22.9 %select_add_fusion.2 = f32[2048,3712]{1,0:T(8,128)} fusion(f32[2048,3712]{1,0:T(8,128)} %get-tuple-element.87, pred[]{:T(512)S(6)} %compare.3, bf16[2,128,3712]{2,1,0:T(8,128)(2,1)} %get-tuple-element.95, s32[]{:T(128)S(6)} %copy.9, bf16[2,128,2048]{1,2,0:T(8,128)(2,1)S(1)} %get-tuple-element.94), kind=kOutput, calls=%fused_computation.clone.1 | convolution fusion | flops 1976565760 | bytes 62293504 | tf_op jit(solution)/shard_map/while/body/eval_jaxpr/dot_general | solution.py:17
  86.6 15.9 %convert_element_type.27 = bf16[2048,3712]{1,0:T(8,128)(2,1)} convert(f32[2048,3712]{1,0:T(8,128)} %get-tuple-element.27) | non-fusion elementwise | flops 7602176 | bytes 45613056 | tf_op jit(solution)/shard_map/convert_element_type | solution.py:34
  102.5 0.0 all-reduce.2.cloned.1.call-update
  102.6 511.4 %all-reduce.2.cloned.1.call-done = bf16[2048,3712]{1,0:T(8,128)(2,1)} async-done(((bf16[2048,3712]{1,0:T(8,128)(2,1)}), bf16[2048,3712]{1,0:T(8,128)(2,1)}) %all-reduce.2.cloned.1.call-update) | async-done | bytes 15204368 | tf_op jit(solution)/shard_map/psum | solution.py:34
  614.0 13.7 %fusion.5 = f32[]{:T(128)} fusion(bf16[2048,3712]{1,0:T(8,128)(2,1)} %all-reduce.2.cloned.1.call-done), kind=kLoop, calls=%fused_computation.8 | loop fusion | flops 22806528 | bytes 15204356 | tf_op jit(solution)/shard_map/reduce_sum | solution.py:35
  627.7 14.1 %psum.15 = f32[]{:T(128)} all-reduce(f32[]{:T(128)} %fusion.5), channel_id=1, replica_groups=mesh['rep'=4,'fsdp'=2,'tp'=4] {'fsdp','tp'}, use_global_device_ids=true, to_apply=%region_4.5 | all-reduce | flops 1 | bytes 8 | tf_op jit(solution)/shard_map/psum | solution.py:35
  642.5 11.4 %fusion.6 = bf16[2048,3712]{1,0:T(8,128)(2,1)} fusion(bf16[2048,3712]{1,0:T(8,128)(2,1)} %all-reduce.2.cloned.1.call-done, f32[]{:T(128)S(6)} %sqrt.3), kind=kLoop, calls=%fused_computation.9 | loop fusion | flops 22806528 | bytes 30408708 | tf_op jit(solution)/shard_map/convert_element_type | solution.py:38
  (1 shorter events, 0.0 us)
Async XLA Ops:
  6.5 44.6 %all-gather.2.cloned.1.call-start = ((), (), s32[]{:S(2)}) async-start(), calls=%async_computation.1 | async-start | bytes 2850816 | tf_op jit(solution)/shard_map/all_gather | solution.py:22
  11.8 27.3 %all-to-all-start = ((bf16[128,2,2048]{0,2,1:T(8,128)(2,1)}), bf16[128,2,2048]{0,2,1:T(8,128)(2,1)S(1)}, u32[]{:S(2)}, u32[]{:S(2)}) async-start(bf16[128,2,2048]{0,2,1:T(8,128)(2,1)} %bitcast), calls=%async_computation | async-start | bytes 2097152 | tf_op jit(solution)/shard_map/all_to_all | solution.py:13
  16.1 597.9 %all-reduce.2.cloned.1.call-start = ((), (), s32[]{:S(2)}) async-start(), calls=%async_computation.2 | async-start | bytes 30408704 | tf_op jit(solution)/shard_map/psum | solution.py:34
Sparse Core Ops, SparseCore 0:
  9.7 41.3 all-gather.1
  102.7 511.2 all-reduce.1
where the time goes:
time: 661 us
  waiting for transfers between devices  546 us (83%)
  other arithmetic  44.1 us (7%)
  matrix products  35.5 us (5%)
  blocking collectives  14.1 us (2%)
  between operations  14.1 us (2%)
    psum x1, waiting for transfers between devices, on_device(): summed = lax.psum(running.astype(jnp.bfloat16), 'rep').astype(jnp.float32)  511 us
    dot_general x2, matrix products, advance(): jnp.dot(grad_rows.T, hidden_rows, preferred_element_type=jnp.float32)  35.5 us
    all_to_all x1, waiting for transfers between devices, on_device(): lax.all_to_all(out_grad, 'fsdp', split_axis=1, concat_axis=0, tiled=True)  23 us
    convert_element_type x1, other arithmetic, on_device(): summed = lax.psum(running.astype(jnp.bfloat16), 'rep').astype(jnp.float32)  15.9 us
    psum x1, blocking collectives, on_device(): square_total = lax.psum(jnp.sum(summed * summed), ('fsdp', 'tp'))  14.1 us
    reduce_sum x1, other arithmetic, on_device(): square_total = lax.psum(jnp.sum(summed * summed), ('fsdp', 'tp'))  13.7 us
  transfers between devices with their start and end apart: 3, of which 3 were waited for; matrix products, arithmetic and copies ran while one was open for 0% of the time, Pallas kernels for 0%

commit v1 on v0

--- a/solution.py
+++ b/solution.py
@@ -2,6 +2,11 @@
 import jax.numpy as jnp
 from jax import lax
 from jax.sharding import PartitionSpec as P
+
+
+def add_all(array, mesh_axis):
+    shards = lax.all_gather(array, mesh_axis)
+    return jnp.sum(shards, axis=0)
 
 
 def on_device(gate_pre, up_pre, out_grad):
@@ -31,7 +36,7 @@
             portion.reshape(blocks, block_rows, portion.shape[1]),
         ),
     )
-    summed = lax.psum(running.astype(jnp.bfloat16), "rep").astype(jnp.float32)
+    summed = add_all(running.astype(jnp.bfloat16), "rep").astype(jnp.float32)
     square_total = lax.psum(jnp.sum(summed * summed), ("fsdp", "tp"))
     entry_count = summed.shape[0] * lax.axis_size("fsdp") * summed.shape[1] * lax.axis_size("tp")
     factor = 1.0 / jnp.sqrt(square_total / entry_count + 1e-06)

time: 661 us -> 1190 us (1.80)
  waiting for transfers between devices: 546 us -> 1040 us
  other arithmetic: 44.1 us -> 72.6 us
    all_gather x0 -> x1, waiting for transfers between devices: none -> 1010 us  [add_all(): shards = lax.all_gather(array, mesh_axis)]
    psum x1 -> x0, waiting for transfers between devices: 511 us -> none  [on_device(): summed = lax.psum(running.astype(jnp.bfloat16), 'rep').astype(jnp.float32)]
    reduce_sum x0 -> x1, other arithmetic: none -> 28.5 us  [add_all(): return jnp.sum(shards, axis=0)]
where the time goes in v1:
time: 1190 us
  waiting for transfers between devices  1040 us (87%)
  other arithmetic  72.6 us (6%)
  matrix products  35.5 us (3%)
  blocking collectives  14.4 us (1%)
  between operations  14 us (1%)
    all_gather x1, waiting for transfers between devices, add_all(): shards = lax.all_gather(array, mesh_axis)  1010 us
    dot_general x2, matrix products, advance(): jnp.dot(grad_rows.T, hidden_rows, preferred_element_type=jnp.float32)  35.5 us
    reduce_sum x1, other arithmetic, add_all(): return jnp.sum(shards, axis=0)  28.5 us
  transfers between devices with their start and end apart: 3, of which 3 were waited for; matrix products, arithmetic and copies ran while one was open for 0% of the time, Pallas kernels for 0%

profile of v1, /device:TPU:0, one launch (start us, length us, event | category | flops | bytes accessed | tf_op | source)
XLA Modules:
  0.0 1187.1 jit_solution(812235288750005157)
XLA Ops:
  6.5 0.0 all-gather.4.cloned.1.call-start
  6.5 3.0 fusion.11
  9.5 0.0 all-gather.4.cloned.1.call-update
  9.6 2.3 copy.4
  11.8 4.2 all-to-all-start
  16.1 0.0 all-gather.6.cloned.1.call-start
  16.1 23.0 %all-to-all-done = bf16[128,2,2048]{0,2,1:T(8,128)(2,1)S(1)} async-done(((bf16[128,2,2048]{0,2,1:T(8,128)(2,1)}), bf16[128,2,2048]{0,2,1:T(8,128)(2,1)S(1)}, u32[]{:S(2)}, u32[]{:S(2)}) %all-to-all-start) | async-done | bytes 1048608 | tf_op jit(solution)/shard_map/all_to_all | solution.py:18
  39.1 12.0 %all-gather.4.cloned.1.call-done = bf16[256,3712]{1,0:T(8,128)(2,1)} async-done(((bf16[128,3712]{1,0:T(8,128)(2,1)}), bf16[256,3712]{1,0:T(8,128)(2,1)}) %all-gather.4.cloned.1.call-update) | async-done | bytes 1900560 | tf_op jit(solution)/shard_map/all_gather | solution.py:27
  51.1 35.5 %while.11 = (s32[]{:T(128)}, f32[2048,3712]{1,0:T(8,128)}, bf16[2,128,2048]{1,2,0:T(8,128)(2,1)S(1)}, bf16[2,128,3712]{2,1,0:T(8,128)(2,1)}, s32[]{:T(128)}, /*index=5*/s32[]{:T(128)}) while((s32[]{:T(128)}, f32[2048,3712]{1,0:T(8,128)}, bf16[2,128,2048]{1,2,0:T(8,128)(2,1)S(1)}, bf16[2,128,3712]{2,1,0:T(8,128)(2,1)}, s32[]{:T(128)}, ...), condition=%wide.region_1.2_spmd.clone, body=%wide.region_0.1_spmd.clone.sunk | while | flops 1976565760 | bytes 62293588 | solution.py:31
  51.1 12.6 %select_add_fusion.2 = f32[2048,3712]{1,0:T(8,128)} fusion(f32[2048,3712]{1,0:T(8,128)} %get-tuple-element.87, pred[]{:T(512)S(6)} %compare.3, bf16[2,128,3712]{2,1,0:T(8,128)(2,1)} %get-tuple-element.95, s32[]{:T(128)S(6)} %copy.9, bf16[2,128,2048]{1,2,0:T(8,128)(2,1)S(1)} %get-tuple-element.94), kind=kOutput, calls=%fused_computation.clone.1 | convolution fusion | flops 1976565760 | bytes 62293504 | tf_op jit(solution)/shard_map/while/body/eval_jaxpr/dot_general | solution.py:22
  63.7 22.9 %select_add_fusion.2 = f32[2048,3712]{1,0:T(8,128)} fusion(f32[2048,3712]{1,0:T(8,128)} %get-tuple-element.87, pred[]{:T(512)S(6)} %compare.3, bf16[2,128,3712]{2,1,0:T(8,128)(2,1)} %get-tuple-element.95, s32[]{:T(128)S(6)} %copy.9, bf16[2,128,2048]{1,2,0:T(8,128)(2,1)S(1)} %get-tuple-element.94), kind=kOutput, calls=%fused_computation.clone.1 | convolution fusion | flops 1976565760 | bytes 62293504 | tf_op jit(solution)/shard_map/while/body/eval_jaxpr/dot_general | solution.py:22
  86.6 15.9 %convert_element_type.29 = bf16[2048,3712]{1,0:T(8,128)(2,1)} convert(f32[2048,3712]{1,0:T(8,128)} %get-tuple-element.27) | non-fusion elementwise | flops 7602176 | bytes 45613056 | tf_op jit(solution)/shard_map/convert_element_type | solution.py:39
  102.5 0.0 all-gather.6.cloned.1.call-update
  102.6 1009.1 %all-gather.6.cloned.1.call-done = bf16[8192,3712]{1,0:T(8,128)(2,1)} async-done(((bf16[2048,3712]{1,0:T(8,128)(2,1)}), bf16[8192,3712]{1,0:T(8,128)(2,1)}) %all-gather.6.cloned.1.call-update) | async-done | bytes 60817424 | tf_op jit(solution)/shard_map/all_gather | solution.py:8
  1111.7 28.5 %reduce_sum.21 = bf16[2048,3712]{1,0:T(8,128)(2,1)} reduce(bf16[4,2048,3712]{2,1,0:T(8,128)(2,1)} %bitcast.15, bf16[]{:T(256)} %constant.22.clone.1), dimensions={0}, to_apply=%region_2.3 | reduce | flops 22806528 | bytes 76021760 | tf_op jit(solution)/shard_map/reduce_sum | solution.py:9
  1140.1 13.7 %fusion.5 = f32[]{:T(128)} fusion(bf16[2048,3712]{1,0:T(8,128)(2,1)} %reduce_sum.21), kind=kLoop, calls=%fused_computation.8 | loop fusion | flops 22806528 | bytes 15204356 | tf_op jit(solution)/shard_map/reduce_sum | solution.py:40
  1153.9 14.4 %psum.7 = f32[]{:T(128)} all-reduce(f32[]{:T(128)} %fusion.5), channel_id=1, replica_groups=mesh['rep'=4,'fsdp'=2,'tp'=4] {'fsdp','tp'}, use_global_device_ids=true, to_apply=%region_4.5 | all-reduce | flops 1 | bytes 8 | tf_op jit(solution)/shard_map/psum | solution.py:40
  1168.9 11.4 fusion.6
  (1 shorter events, 0.0 us)
Async XLA Ops:
  6.5 44.6 %all-gather.4.cloned.1.call-start = ((), (), s32[]{:S(2)}) async-start(), calls=%async_computation.1 | async-start | bytes 2850816 | tf_op jit(solution)/shard_map/all_gather | solution.py:27
  11.8 27.3 %all-to-all-start = ((bf16[128,2,2048]{0,2,1:T(8,128)(2,1)}), bf16[128,2,2048]{0,2,1:T(8,128)(2,1)S(1)}, u32[]{:S(2)}, u32[]{:S(2)}) async-start(bf16[128,2,2048]{0,2,1:T(8,128)(2,1)} %bitcast), calls=%async_computation | async-start | bytes 2097152 | tf_op jit(solution)/shard_map/all_to_all | solution.py:18
  16.1 1095.6 %all-gather.6.cloned.1.call-start = ((), (), s32[]{:S(2)}) async-start(), calls=%async_computation.2 | async-start | bytes 76021760 | tf_op jit(solution)/shard_map/all_gather | solution.py:8
Sparse Core Ops, SparseCore 0:
  9.7 41.3 all-gather.3
  102.7 1008.9 all-gather.5
